TPU v7x, 32 devices: a whole 2x2x4 slice. The times are simulated.
32 devices in a mesh: dp: 8 (over z, y), mp: 4 (over x, core).
Axes of the slice: x: 2, y: 2, z: 4, core: 2. Of those that a mesh axis runs over, the one named last changes fastest.
Arguments:
- pred_input: bfloat16 [512, 256, 384], P('dp'), may hold values from -6 to 6
- proj_weight: bfloat16 [384, 1280], P('dp', 'mp'), may hold values from -0.3125 to 0.3125
- proj_bias: float32 [1280], P('mp'), may hold values from -3 to 3
- targets: bfloat16 [512, 256, 1280], P('dp', None, 'mp'), may hold values from -6 to 6
- block_masks: int32 [512, 4, 256], P('dp'), may hold values from 0 to 1, as said below
Outputs:
- loss: float32 [], replicated
- clip_scale: float32 [], replicated
- grad_weight: float32 [384, 1280], P('dp', 'mp')
- grad_bias: float32 [1280], P('mp')
Inputs may be any that keep to these rules, and one draw needn't show every extreme that they name: `block_masks`: each of an image's 4 target blocks is a nonempty rectangle of patches on the 16 x 16 grid (row-major patch order); blocks may intersect.
All inputs are finite; a program needn't handle non-finite values.
Results may differ from a plain program's by a relative error of at most 0.0003.
Values may be sent and summed in bfloat16 or wider, within the bound.
A program may use at most 192 MiB of HBM per device.

v0:
```python
import jax
import jax.numpy as jnp
from jax import lax
from jax.sharding import PartitionSpec as P


def body(pred_input, proj_weight, proj_bias, targets, block_masks):
    images_here, patches, pred_width = pred_input.shape
    feat_local = targets.shape[2]
    feat_full = feat_local * lax.axis_size("mp")
    token_count = images_here * patches
    coverage = jnp.sum(block_masks, axis=1).astype(jnp.float32)
    share = patches // lax.axis_size("mp")
    owned_cover = lax.dynamic_slice_in_dim(coverage, lax.axis_index("mp") * share, share, 1)
    count_part = jnp.sum(owned_cover)
    target_f = targets.astype(jnp.float32).reshape(token_count, feat_local)
    feat_sums, feat_squares = lax.psum(
        (jnp.sum(target_f, axis=1), jnp.sum(target_f * target_f, axis=1)), "mp"
    )
    mean_feat = feat_sums / feat_full
    variance = feat_squares / feat_full - mean_feat * mean_feat
    tnorm = (target_f - mean_feat[:, None]) * lax.rsqrt(variance[:, None] + 1e-05)
    inputs_flat = pred_input.reshape(token_count, pred_width)
    weight_full = lax.all_gather(proj_weight, "dp", axis=0, tiled=True)
    pred = jnp.dot(inputs_flat, weight_full, preferred_element_type=jnp.float32) + proj_bias
    differ = pred - tnorm
    magnitude = jnp.abs(differ)
    smooth = jnp.where(magnitude < 1.0, 0.5 * differ * differ, magnitude - 0.5)
    cover_column = coverage.reshape(token_count, 1)
    loss_part = jnp.sum(cover_column * smooth)
    clipped = cover_column * jnp.clip(differ, -1.0, 1.0)
    source = clipped.astype(jnp.bfloat16)
    grad_full = lax.dot_general(
        inputs_flat, source, (((0,), (0,)), ((), ())), preferred_element_type=jnp.float32
    )
    bias_part = jnp.sum(clipped, axis=0)
    grad_rows = lax.psum_scatter(grad_full, "dp", scatter_dimension=0, tiled=True)
    bias_grad = lax.psum(bias_part, "dp")
    bias_square = jnp.where(lax.axis_index("dp") == 0, jnp.sum(bias_grad * bias_grad), 0.0)
    square_part = jnp.sum(grad_rows * grad_rows) + bias_square
    total = lax.psum(count_part, ("dp", "mp"))
    loss_total = lax.psum(loss_part, ("dp", "mp"))
    square_total = lax.psum(square_part, ("dp", "mp"))
    norm = jnp.sqrt(square_total) / total
    clip_scale = jnp.minimum(1.0, 1.0 / (norm + 1e-06))
    factor = clip_scale / total
    loss = loss_total / total / feat_full
    return (loss, clip_scale, grad_rows * factor, bias_grad * factor)


def solution(mesh):
    in_specs = (
        P("dp", None, None),
        P("dp", "mp"),
        P("mp"),
        P("dp", None, "mp"),
        P("dp", None, None),
    )
    out_specs = (P(), P(), P("dp", "mp"), P("mp"))
    return jax.shard_map(body, mesh=mesh, in_specs=in_specs, out_specs=out_specs, check_vma=False)
```

profile of v0, /device:TPU:0, one launch (start us, length us, event | category | flops | bytes accessed | tf_op | source)
XLA Modules:
  0.0 243.8 jit_solution(10438953832590673611)
XLA Ops:
  7.2 0.0 all-reduce.4.cloned.1.call-start
  7.2 9.9 %convert_reduce_fusion = (f32[64,256]{1,0:T(8,128)S(1)}, f32[64,256]{1,0:T(8,128)S(1)}) fusion(bf16[64,256,320]{1,2,0:T(8,128)(2,1)} %param.8), kind=kLoop, calls=%fused_computation.2 | loop fusion | flops 20938752 | bytes 10616832 | tf_op jit(solution)/shard_map/reduce_sum | solution.py:18
  17.2 0.7 copy.19
  17.8 0.7 copy.20
  18.5 0.0 all-reduce.4.cloned.1.call-update
  18.5 0.0 reduce-scatter.4.cloned.1.call-start
  18.5 13.9 %convert_bitcast_fusion = f32[64,40,8,256]{3,2,1,0:T(8,128)} fusion(bf16[64,256,320]{1,2,0:T(8,128)(2,1)} %param.8), kind=kLoop, calls=%fused_computation.3 | loop fusion | flops 5242880 | bytes 31457280
  32.4 0.2 reduce_sum.76
  32.7 15.9 %copy.17 = f32[64,40,8,256]{3,2,0,1:T(8,128)} copy(f32[64,40,8,256]{3,2,1,0:T(8,128)} %convert_bitcast_fusion) | data formatting | bytes 41943040 | tf_op jit(solution)/shard_map/reshape | solution.py:16
  48.6 32.7 %all_gather.3 = bf16[384,320]{1,0:T(8,128)(2,1)S(1)} all-gather(bf16[48,320]{1,0:T(8,128)(2,1)S(1)} %copy-done.1), channel_id=1, replica_groups=mesh['dp'=8,'mp'=4] {'dp'}, dimensions={0}, use_global_device_ids=true | all-gather | bytes 276480 | tf_op jit(solution)/shard_map/all_gather | solution.py:24
  81.3 0.9 broadcast_multiply_fusion.1
  82.2 26.1 %fusion.5 = (f32[320]{0:T(512)S(1)}, f32[]{:T(128)}, f32[16384,320]{0,1:T(8,128)}) fusion(f32[16384]{0:T(1024)S(1)} %bitcast.20, f32[16384]{0:T(1024)S(1)} %get-tuple-element.28, f32[16384,320]{0,1:T(8,128)} %bitcast.19, f32[16384]{0:T(1024)S(1)} %get-tuple-element.27, f32[320]{0:T(512)S(1)} %copy-done.2, bf16[16384,384]{1,0:T(8,128)(2,1)} %bitcast.17, ...), kind=kOutput, calls=%fused_computation.11 | convolution fusion | flops 4105174784 | bytes 54970884 | tf_op jit(solution)/shard_map/dot_general | solution.py:25
  108.3 13.5 %fusion.12 = f32[384,320]{0,1:T(8,128)S(1)} fusion(bf16[16384,384]{1,0:T(8,128)(2,1)} %bitcast.18, f32[16384,320]{0,1:T(8,128)} %get-tuple-element.29, f32[16384]{0:T(1024)S(1)} %bitcast.21), kind=kOutput, calls=%fused_computation.17 | convolution fusion | flops 4042260480 | bytes 34111488 | tf_op jit(solution)/shard_map/dot_general | solution.py:33
  121.8 1.0 copy.15
  122.8 0.0 reduce-scatter.4.cloned.1.call-update
  122.9 0.7 dynamic-slice_reduce_fusion
  123.5 21.5 %psum.46 = f32[320]{0:T(512)S(1)} all-reduce(f32[320]{0:T(512)S(1)} %get-tuple-element.16), channel_id=1, replica_groups=mesh['dp'=8,'mp'=4] {'dp'}, use_global_device_ids=true, to_apply=%region_12.13 | all-reduce | flops 320 | bytes 2560 | tf_op jit(solution)/shard_map/psum | solution.py:38
  145.1 0.6 multiply_reduce_fusion.1
  146.3 40.9 %reduce-scatter.4.cloned.1.call-done = f32[48,320]{1,0:T(8,128)} async-done(((f32[384,320]{1,0:T(8,128)}), f32[48,320]{1,0:T(8,128)}) %reduce-scatter.4.cloned.1.call-update) | async-done | bytes 61456
  187.2 1.0 copy.16
  188.2 0.6 multiply_reduce_fusion
  189.5 40.3 %all-reduce = (f32[]{:T(128)}, f32[]{:T(128)}, f32[]{:T(128)}) all-reduce(f32[]{:T(128)} %get-tuple-element.17, f32[]{:T(128)} %dynamic-slice_reduce_fusion, f32[]{:T(128)S(6)} %add.44), channel_id=1, replica_groups=mesh['dp'=8,'mp'=4] {'dp','mp'}, use_global_device_ids=true, to_apply=%region_6.7 | all-reduce | flops 3 | bytes 24 | tf_op jit(solution)/shard_map/psum | solution.py:42
  232.0 0.6 broadcast_multiply_fusion.2
  233.9 0.7 copy.14
  (10 shorter events, 0.1 us)
Async XLA Ops:
  7.2 25.3 %copy-start = (s32[64,4,256]{2,1,0:T(4,128)S(1)}, s32[64,4,256]{2,1,0:T(4,128)}, u32[]{:S(2)}) copy-start(s32[64,4,256]{2,1,0:T(4,128)} %param.9) | copy-start | bytes 786436
  7.2 74.2 %all-reduce.4.cloned.1.call-start = ((), (), s32[]{:S(2)}) async-start(), calls=%async_computation.2 | async-start | bytes 262144 | tf_op jit(solution)/shard_map/psum | solution.py:17
  18.5 168.7 %reduce-scatter.4.cloned.1.call-start = ((), (), s32[]{:S(2)}) async-start(), calls=%async_computation.1 | async-start | bytes 663552
  32.7 16.0 %copy-start.1 = (bf16[48,320]{1,0:T(8,128)(2,1)S(1)}, bf16[48,320]{1,0:T(8,128)(2,1)}, u32[]{:S(2)}) copy-start(bf16[48,320]{1,0:T(8,128)(2,1)} %param.6) | copy-start | bytes 92164
  32.7 49.6 %copy-start.2 = (f32[320]{0:T(512)S(1)}, f32[320]{0:T(512)}, u32[]{:S(2)}) copy-start(f32[320]{0:T(512)} %param.7) | copy-start | bytes 3844
Sparse Core Ops, SparseCore 0:
  18.6 34.5 all-reduce.3
  123.0 64.2 reduce-scatter.3
where the time goes:
time: 244 us
  blocking collectives  94.6 us (39%)
  waiting for transfers between devices  41 us (17%)
  matrix products  39.5 us (16%)
  other arithmetic  27.4 us (11%)
  between operations  21.1 us (9%)
  local copies, waits for them, and re-layouts  20.1 us (8%)
    unnamed x3, waiting for transfers between devices  41 us
    psum x1, blocking collectives, body(): loss_total = lax.psum(loss_part, ('dp', 'mp'))  40.3 us
    all_gather x1, blocking collectives, body(): weight_full = lax.all_gather(proj_weight, 'dp', axis=0, tiled=True)  32.7 us
    dot_general x1, matrix products, body(): jnp.dot(inputs_flat, weight_full, preferred_element_type=jnp.float32)  26.1 us
    psum x1, blocking collectives, body(): bias_grad = lax.psum(bias_part, 'dp')  21.5 us
    reshape x1, local copies, waits for them, and re-layouts, body(): target_f = targets.astype(jnp.float32).reshape(token_count, feat_local)  15.9 us
    unnamed x1, other arithmetic  13.9 us
    dot_general x1, matrix products, body(): lax.dot_general(inputs_flat, source, (((0,), (0,)), ((), ())), preferred_...  13.5 us
  transfers between devices with their start and end apart: 2, of which 1 were waited for; matrix products, arithmetic and copies ran while one was open for 13% of the time, Pallas kernels for 0%

commit v1 on v0

v1 whole, which is shorter than its diff:
```python
import functools

import jax
import jax.numpy as jnp
from jax import lax
from jax.experimental import pallas as pl
from jax.experimental.pallas import tpu as pltpu
from jax.sharding import PartitionSpec as P

F32 = jnp.float32
BF16 = jnp.bfloat16
MESH = pl.DeviceIdType.MESH
LANES = 128
GROUP = 8
PAIR = 2
CHUNK = 16


def pad_to(n, m):
    return (n + m - 1) // m * m


def kernel(ndp, nmp, x_hbm, w_ref, b_ref, t_hbm, m_hbm,
           loss_ref, clip_ref, gw_ref, gb_ref,
           xv, tv, mv, wall, wfull, wt, bcol, brow, ssend, srecv, rbuf, mbuf, cbuf,
           pa, pb, sa, sb, acc, gacc, lacc, gsend, grecv, fsend, frecv,
           xsem, tsem, msem, wss, wrs, sss, srs, gss, grs, fss, frs):
    images, feat, patches = tv.shape
    width = xv.shape[1]
    rows = w_ref.shape[0]
    rows_pad = gsend.shape[1] - 8
    featp = acc.shape[0]
    groups = images // GROUP
    ntot = ndp * nmp
    dp, mp = lax.axis_index("dp"), lax.axis_index("mp")
    me = dp * nmp + mp
    feat_full = feat * nmp

    def t_copy(g):
        s = pl.ds(g * GROUP, GROUP)
        return pltpu.make_async_copy(t_hbm.at[s], tv.at[s], tsem.at[g])

    def x_copy(g):
        s = pl.ds(g * GROUP * patches, GROUP * patches)
        return pltpu.make_async_copy(x_hbm.at[s], xv.at[s], xsem.at[g])

    m_copy = pltpu.make_async_copy(m_hbm, mv, msem)

    barrier = pltpu.get_barrier_semaphore()

    def greet(o, _):
        d = lax.rem(me + o, ntot)
        pl.semaphore_signal(barrier, inc=1, device_id=(d // nmp, lax.rem(d, nmp)), device_id_type=MESH)
        return 0

    lax.fori_loop(1, ntot, greet, 0)
    m_copy.start()
    for g in range(groups):
        t_copy(g).start()
    for g in range(groups):
        x_copy(g).start()

    acc[...] = jnp.zeros_like(acc)
    gacc[...] = jnp.zeros_like(gacc)
    lacc[...] = jnp.zeros_like(lacc)
    sb[...] = jnp.zeros_like(sb)
    wfull[...] = jnp.zeros_like(wfull)
    brow[...] = jnp.zeros_like(brow)
    brow[0:1, :feat] = b_ref[...]
    bcol[...] = jnp.transpose(jnp.broadcast_to(brow[0:1, :], (LANES, featp)))

    pl.semaphore_wait(barrier, ntot - 1)

    def w_copy(o):
        return pltpu.make_async_remote_copy(
            src_ref=w_ref, dst_ref=wall.at[o - 1], send_sem=wss.at[o - 1], recv_sem=wrs.at[o - 1],
            device_id=(lax.rem(dp + o, ndp), mp), device_id_type=MESH)

    for o in range(1, ndp):
        w_copy(o).start()

    def s_copy(o, g):
        return pltpu.make_async_remote_copy(
            src_ref=ssend.at[g], dst_ref=srecv.at[o - 1, g],
            send_sem=sss.at[o - 1, g], recv_sem=srs.at[o - 1, g],
            device_id=(dp, lax.rem(mp + o, nmp)), device_id_type=MESH)

    m_copy.wait()

    def cover(g, _):
        block = [jnp.sum(mv[g * GROUP + j], axis=0, keepdims=True) for j in range(GROUP)]
        cbuf[pl.ds(pl.multiple_of(g * GROUP, GROUP), GROUP), :] = jnp.concatenate(block, axis=0).astype(F32)
        return 0

    lax.fori_loop(0, groups, cover, 0)

    def stats(g, _):
        t_copy(g).wait()

        sums, squares = [], []
        for j in range(GROUP):
            i = g * GROUP + j
            part = jnp.zeros((CHUNK, patches), F32)
            for c in range(0, feat, CHUNK):
                part = part + tv[i, c:c + CHUNK, :].astype(F32)
            total = jnp.sum(part, axis=0, keepdims=True)
            mean = total * (1.0 / feat)
            part = jnp.zeros((CHUNK, patches), F32)
            for c in range(0, feat, CHUNK):
                centred = tv[i, c:c + CHUNK, :].astype(F32) - mean
                part = part + centred * centred
            sums.append(total)
            squares.append(jnp.sum(part, axis=0, keepdims=True))
        ssend[g] = jnp.concatenate(sums + squares, axis=0)

        @pl.when(g > 0)
        def _():
            for o in range(1, nmp):
                s_copy(o, g - 1).start()

        return 0

    lax.fori_loop(0, groups, stats, 0)

    def place(owner_static, block):
        wfull[owner_static * rows:(owner_static + 1) * rows, :feat] = block.astype(F32)

    for o in range(1, ndp):
        w_copy(o).wait_recv()
    for o in range(1, nmp):
        s_copy(o, groups - 1).start()
    for k in range(ndp):
        slot = lax.rem(dp - k + ndp, ndp)
        other = wall[jnp.maximum(slot - 1, 0)].astype(F32)
        mine = w_ref[...].astype(F32)
        place(k, jnp.where(slot == 0, mine, other))
    wt[...] = jnp.transpose(wfull[...])[:feat].astype(BF16)

    def x_rows(k):
        n = PAIR * patches
        return xv[pl.ds(pl.multiple_of(k * n, n), n), :]

    def project(p_ref, k):
        p_ref[...] = lax.dot_general(wt[...], x_rows(k), (((1,), (1,)), ((), ())), preferred_element_type=F32)

    def gradient(s_ref, k):
        acc[:feat, :] += jnp.dot(s_ref[...], x_rows(k), preferred_element_type=F32)

    def pointwise(p_ref, s_ref, k):
        img = k * PAIR
        rs = [rbuf[pl.ds(img + g, 1), :] for g in range(PAIR)]
        ms = [mbuf[pl.ds(img + g, 1), :] for g in range(PAIR)]
        cs = [cbuf[pl.ds(img + g, 1), :] for g in range(PAIR)]
        loss = jnp.zeros((CHUNK, patches), F32)
        for c in range(0, feat, CHUNK):
            bias = bcol[c:c + CHUNK, :]
            bias = jnp.concatenate([bias] * (patches // LANES), axis=1)
            total = jnp.zeros((CHUNK, LANES), F32)
            for g in range(PAIR):
                cols = slice(g * patches, (g + 1) * patches)
                t = tv[img + g, c:c + CHUNK, :].astype(F32)
                differ = (p_ref[c:c + CHUNK, cols] + bias) + (ms[g] - t * rs[g])
                clipped = jnp.clip(differ, -1.0, 1.0)
                source = clipped * cs[g]
                loss = loss + source * (differ - 0.5 * clipped)
                for h in range(0, patches, LANES):
                    total = total + source[:, h:h + LANES]
                s_ref[c:c + CHUNK, cols] = source.astype(BF16)
            gacc[c:c + CHUNK, :] += total
        lacc[...] += loss

    x_copy(0).wait()
    project(pa, 0)
    steps = images // PAIR
    per_group = GROUP // PAIR

    def outer(g, _):
        @pl.when(g + 1 < groups)
        def _():
            x_copy(g + 1).wait()

        for o in range(1, nmp):
            s_copy(o, g).wait_recv()
        parts = [ssend[g]] + [srecv[o - 1, g] for o in range(1, nmp)]
        sums = [p[:GROUP] for p in parts]
        mean = functools.reduce(jnp.add, sums) * (1.0 / feat_full)
        var = functools.reduce(jnp.add, [p[GROUP:] for p in parts])
        for s in sums:
            gap = s * (1.0 / feat) - mean
            var = var + feat * (gap * gap)
        rstd = lax.rsqrt(var * (1.0 / feat_full) + 1e-05)
        here = pl.ds(pl.multiple_of(g * GROUP, GROUP), GROUP)
        rbuf[here, :] = rstd
        mbuf[here, :] = mean * rstd

        def inner(j, _):
            k = g * per_group + 2 * j
            pointwise(pa, sa, k)
            project(pb, k + 1)
            gradient(sb, jnp.maximum(k - 1, 0))
            pointwise(pb, sb, k + 1)
            project(pa, jnp.minimum(k + 2, steps - 1))
            gradient(sa, k)
            return 0

        lax.fori_loop(0, per_group // 2, inner, 0)
        return 0

    lax.fori_loop(0, groups, outer, 0)
    gradient(sb, steps - 1)

    bias_part = jnp.sum(jnp.transpose(gacc[...]), axis=0, keepdims=True)
    loss_part = jnp.sum(lacc[...], keepdims=True)
    count_part = jnp.sum(cbuf[...], keepdims=True)
    row_of = lax.broadcasted_iota(jnp.int32, (8, featp), 0)
    extra = jnp.where(row_of == 0, bias_part, jnp.where(row_of == 1, loss_part, count_part))
    full = jnp.transpose(acc[...])
    for k in range(ndp):
        gsend[k, :rows, :] = full[k * rows:(k + 1) * rows, :]
        gsend[k, rows_pad:, :] = extra

    def g_copy(o):
        to = lax.rem(dp + o, ndp)
        return pltpu.make_async_remote_copy(
            src_ref=gsend.at[to], dst_ref=grecv.at[o - 1],
            send_sem=gss.at[o - 1], recv_sem=grs.at[o - 1],
            device_id=(to, mp), device_id_type=MESH)

    for o in range(1, ndp):
        g_copy(o).start()
    grad = gsend[dp, :rows, :]
    sums = gsend[dp, rows_pad:, :]
    for o in range(1, ndp):
        g_copy(o).wait_recv()
        grad = grad + grecv[o - 1, :rows, :]
        sums = sums + grecv[o - 1, rows_pad:, :]
    bias_grad = sums[0:1, :]
    square = jnp.sum(grad * grad, keepdims=True)
    bias_square = jnp.sum(bias_grad * bias_grad, keepdims=True)
    row_of = lax.broadcasted_iota(jnp.int32, (8, LANES), 0)
    fsend[...] = jnp.where(row_of == 0, square + bias_square * (1.0 / ndp), sums[1:2, :LANES])

    def f_copy(o):
        d = lax.rem(me + o, ntot)
        return pltpu.make_async_remote_copy(
            src_ref=fsend, dst_ref=frecv.at[o - 1], send_sem=fss.at[o - 1], recv_sem=frs.at[o - 1],
            device_id=(d // nmp, lax.rem(d, nmp)), device_id_type=MESH)

    def f_start(o, _):
        f_copy(o).start()
        return 0

    def f_wait(o, _):
        f_copy(o).wait_recv()
        return 0

    lax.fori_loop(1, ntot, f_start, 0)
    count = sums[2:3, :LANES]
    lax.fori_loop(1, ntot, f_wait, 0)
    final = fsend[...] + jnp.sum(frecv[...], axis=0)
    norm = jnp.sqrt(final[0:1, :]) / count
    scale = jnp.minimum(1.0, 1.0 / (norm + 1e-06))
    factor = scale / count
    loss = final[1:2, :] / count * (1.0 / (feat_full * ndp))
    loss_ref[...] = loss
    clip_ref[...] = scale
    wide = jnp.concatenate([factor] * (featp // LANES), axis=1)
    gw_ref[...] = (grad * wide)[:, :feat]
    gb_ref[...] = (bias_grad * wide)[:, :feat]

    for o in range(1, ndp):
        w_copy(o).wait_send()
        g_copy(o).wait_send()

    def s_drain(g, _):
        for o in range(1, nmp):
            s_copy(o, g).wait_send()
        return 0

    def f_drain(o, _):
        f_copy(o).wait_send()
        return 0

    lax.fori_loop(0, groups, s_drain, 0)
    lax.fori_loop(1, ntot, f_drain, 0)


def body(pred_input, proj_weight, proj_bias, targets, block_masks):
    images, patches, width = pred_input.shape
    feat = targets.shape[2]
    rows = proj_weight.shape[0]
    blocks = block_masks.shape[1]
    ndp, nmp = lax.axis_size("dp"), lax.axis_size("mp")
    ntot = ndp * nmp
    featp = pad_to(feat, LANES)
    rows_pad = pad_to(rows, 8)
    groups = images // GROUP
    dma = pltpu.SemaphoreType.DMA
    vmem = pl.BlockSpec(memory_space=pltpu.VMEM)
    hbm = pl.BlockSpec(memory_space=pl.ANY)
    loss, clip, gw, gb = pl.pallas_call(
        functools.partial(kernel, ndp, nmp),
        out_shape=(
            jax.ShapeDtypeStruct((1, LANES), F32),
            jax.ShapeDtypeStruct((1, LANES), F32),
            jax.ShapeDtypeStruct((rows, feat), F32),
            jax.ShapeDtypeStruct((1, feat), F32),
        ),
        in_specs=[hbm, vmem, vmem, hbm, hbm],
        out_specs=(vmem,) * 4,
        scratch_shapes=[
            pltpu.VMEM((images * patches, width), BF16),
            pltpu.VMEM((images, feat, patches), BF16),
            pltpu.VMEM((images, blocks, patches), jnp.int32),
            pltpu.VMEM((ndp - 1, rows, feat), BF16),
            pltpu.VMEM((width, featp), F32),
            pltpu.VMEM((feat, width), BF16),
            pltpu.VMEM((featp, LANES), F32),
            pltpu.VMEM((8, featp), F32),
            pltpu.VMEM((groups, 2 * GROUP, patches), F32),
            pltpu.VMEM((nmp - 1, groups, 2 * GROUP, patches), F32),
            pltpu.VMEM((images, patches), F32),
            pltpu.VMEM((images, patches), F32),
            pltpu.VMEM((images, patches), F32),
            pltpu.VMEM((feat, PAIR * patches), F32),
            pltpu.VMEM((feat, PAIR * patches), F32),
            pltpu.VMEM((feat, PAIR * patches), BF16),
            pltpu.VMEM((feat, PAIR * patches), BF16),
            pltpu.VMEM((featp, width), F32),
            pltpu.VMEM((featp, LANES), F32),
            pltpu.VMEM((CHUNK, patches), F32),
            pltpu.VMEM((ndp, rows_pad + 8, featp), F32),
            pltpu.VMEM((ndp - 1, rows_pad + 8, featp), F32),
            pltpu.VMEM((8, LANES), F32),
            pltpu.VMEM((ntot - 1, 8, LANES), F32),
            dma((groups,)), dma((groups,)), dma(()),
            dma((ndp - 1,)), dma((ndp - 1,)),
            dma((nmp - 1, groups)), dma((nmp - 1, groups)),
            dma((ndp - 1,)), dma((ndp - 1,)),
            dma((ntot - 1,)), dma((ntot - 1,)),
        ],
        compiler_params=pltpu.CompilerParams(
            collective_id=0, has_side_effects=True, vmem_limit_bytes=60 * 1024 * 1024
        ),
    )(
        pred_input.reshape(images * patches, width),
        proj_weight,
        proj_bias.reshape(1, feat),
        jnp.swapaxes(targets, 1, 2),
        block_masks,
    )
    return loss[0, 0], clip[0, 0], gw, gb.reshape(feat)


def solution(mesh):
    in_specs = (
        P("dp", None, None),
        P("dp", "mp"),
        P("mp"),
        P("dp", None, "mp"),
        P("dp", None, None),
    )
    out_specs = (P(), P(), P("dp", "mp"), P("mp"))
    return jax.shard_map(body, mesh=mesh, in_specs=in_specs, out_specs=out_specs, check_vma=False)
```

time: 244 us -> 67.3 us (0.28)
  blocking collectives: 94.6 us -> 0 us
  Pallas kernels: 0 us -> 58.8 us
  waiting for transfers between devices: 41 us -> 0 us
  matrix products: 39.5 us -> 0 us
  other arithmetic: 27.4 us -> 1.26 us
  local copies, waits for them, and re-layouts: 20.1 us -> 2.77 us
  between operations: 21.1 us -> 4.15 us
    psum x2 -> x0, blocking collectives: 61.9 us -> none  [the longest x1 40.3 us: body(): loss_total = lax.psum(loss_part, ('dp', 'mp'))]
    pallas_call x0 -> x1, Pallas kernels: none -> 58.8 us  [body(): pl.pallas_call(functools.partial(kernel, ndp, nmp), out_shape=(jax.ShapeD...]
    unnamed x3 -> x0, waiting for transfers between devices: 41 us -> none
    dot_general x2 -> x0, matrix products: 39.5 us -> none  [the longest x1 26.1 us: body(): jnp.dot(inputs_flat, weight_full, preferred_element_type=jnp.float32)]
    all_gather x1 -> x0, blocking collectives: 32.7 us -> none  [body(): weight_full = lax.all_gather(proj_weight, 'dp', axis=0, tiled=True)]
    reshape x1, local copies, waits for them, and re-layouts: 15.9 us -> 1.25 us  [body(): proj_bias.reshape(1, feat)]
    unnamed x1 -> x0, other arithmetic: 13.9 us -> none
    reduce_sum x5 -> x0, other arithmetic: 12 us -> none  [the longest x1 9.93 us: body(): jnp.sum(target_f, axis=1)]
  transfers between devices with their start and end apart: 2 -> 0, of which waited for: 1 -> 0; matrix products, arithmetic and copies ran while one was open for 13% -> 0% of each run, Pallas kernels for 0% -> 0%
where the time goes in v1:
time: 67.3 us; the launch traced here: 67 us
  Pallas kernels  58.8 us (87%)
  between operations  4.15 us (6%)
  local copies, waits for them, and re-layouts  2.77 us (4%)
  other arithmetic  1.26 us (2%)
    pallas_call x1, Pallas kernels, body(): pl.pallas_call(functools.partial(kernel, ndp, nmp), out_shape=(jax.ShapeD...  58.8 us
    unnamed x1, local copies, waits for them, and re-layouts  1.52 us

profile of v1, /device:TPU:0, one launch (start us, length us, event | category | flops | bytes accessed | tf_op | source)
XLA Modules:
  0.0 67.0 jit_solution(16823878165188087359)
XLA Ops:
  0.6 1.2 %reshape.18.b_ref = f32[1,320]{1,0:T(1,128)} reshape(f32[320]{0:T(512)} %param.7) | data formatting | bytes 2560 | tf_op jit(solution)/shard_map/reshape | solution.py:348
  1.9 58.8 %shard_map.84 = (f32[1,128]{1,0:T(1,128)}, f32[1,128]{1,0:T(1,128)}, f32[48,320]{1,0:T(8,128)}, f32[1,320]{1,0:T(1,128)}) custom-call(bf16[16384,384]{1,0:T(8,128)(2,1)} %bitcast.6, bf16[48,320]{1,0:T(8,128)(2,1)} %w_ref.1, f32[1,320]{1,0:T(1,128)} %reshape.18.b_ref, bf16[64,320,256]{2,1,0:T(8,128)(2,1)} %bitcast.7, s32[64,4,256]{2,1,0:T(4,128)} %m_hbm.1), custom_call_target="tpu_custom_call" | custom-call | tf_op jit(solution)/shard_map/pallas_call | solution.py:301
  60.7 1.3 %reduce = f32[320]{0:T(512)} reduce(f32[1,320]{1,0:T(1,128)} %get-tuple-element.11, f32[]{:T(128)} %constant), dimensions={0}, to_apply=%get-tuple-element.11.reduce_sub_computation | reduce | bytes 2564 | tf_op jit(solution)/shard_map/pallas_call | solution.py:301
  63.2 1.5 %copy.14 = f32[48,320]{1,0:T(8,128)} copy(f32[48,320]{1,0:T(8,128)} %get-tuple-element.18) | data formatting | bytes 122880

commit v2 on v1

--- a/solution.py
+++ b/solution.py
@@ -20,19 +20,57 @@
     return (n + m - 1) // m * m
 
 
+def layout(rows, feat):
+    starts, at = [], 0
+    for _ in range(feat // LANES):
+        starts.append(at)
+        at += pad_to(rows, 8)
+    if feat % LANES:
+        starts.append(at)
+        at += pad_to(rows // 2, 8)
+    starts.append(at)
+    return starts, at + 8
+
+
+def finish(ndp, nmp, sum_ref, fin_ref, loss_ref, clip_ref, gw_ref, gb_ref):
+    rows, feat = gw_ref.shape
+    starts, _ = layout(rows, feat)
+    tiles = pad_to(feat, LANES) // LANES
+    count = sum_ref[starts[-1] + tiles + 1:starts[-1] + tiles + 2, 0:1]
+    square, loss = fin_ref[:, 0:1], fin_ref[:, 1:2]
+    norm = jnp.sqrt(square) / count
+    scale = jnp.minimum(1.0, 1.0 / (norm + 1e-06))
+    factor = scale / count
+    loss_ref[...] = loss / count * (1.0 / (feat * nmp * ndp))
+    clip_ref[...] = scale
+    for n in range(feat // LANES):
+        gw_ref[:, n * LANES:(n + 1) * LANES] = sum_ref[starts[n]:starts[n] + rows, :] * factor
+    half = LANES // 2
+    if feat % LANES:
+        packed = sum_ref[starts[-2]:starts[-2] + rows // 2, :] * factor
+        gw_ref[:rows // 2, feat - half:] = packed[:, :half]
+        gw_ref[rows // 2:, feat - half:] = packed[:, half:]
+    for n in range(tiles):
+        stop = min((n + 1) * LANES, feat)
+        bias = sum_ref[starts[-1] + n:starts[-1] + n + 1, :] * factor
+        gb_ref[:, n * LANES:stop] = bias[:, :stop - n * LANES]
+
+
 def kernel(ndp, nmp, x_hbm, w_ref, b_ref, t_hbm, m_hbm,
-           loss_ref, clip_ref, gw_ref, gb_ref,
+           out_ref, fin_ref,
            xv, tv, mv, wall, wfull, wt, bcol, brow, ssend, srecv, rbuf, mbuf, cbuf,
-           pa, pb, sa, sb, acc, gacc, lacc, gsend, grecv, fsend, frecv,
-           xsem, tsem, msem, wss, wrs, sss, srs, gss, grs, fss, frs):
+           pa, pb, sa, sb, acc, gacc, lacc, gsend, pairv, gmid, grecv, fsend, frecv,
+           xsem, tsem, msem, wss, wrs, sss, srs, pss, prs, gss, grs, fss, frs):
     images, feat, patches = tv.shape
     width = xv.shape[1]
     rows = w_ref.shape[0]
-    rows_pad = gsend.shape[1] - 8
+    dp, mp = lax.axis_index("dp"), lax.axis_index("mp")
+    inner_dp = gsend.shape[0]
+    outer_dp = gsend.shape[1]
+    near, far = lax.rem(dp, inner_dp), dp // inner_dp
     featp = acc.shape[0]
     groups = images // GROUP
     ntot = ndp * nmp
-    dp, mp = lax.axis_index("dp"), lax.axis_index("mp")
     me = dp * nmp + mp
     feat_full = feat * nmp
 
@@ -57,9 +95,6 @@
     m_copy.start()
     for g in range(groups):
         t_copy(g).start()
-    for g in range(groups):
-        x_copy(g).start()
-
     acc[...] = jnp.zeros_like(acc)
     gacc[...] = jnp.zeros_like(gacc)
     lacc[...] = jnp.zeros_like(lacc)
@@ -96,6 +131,10 @@
 
     def stats(g, _):
         t_copy(g).wait()
+
+        @pl.when(g >= 2)
+        def _():
+            x_copy(g - 2).start()
 
         sums, squares = [], []
         for j in range(GROUP):
@@ -121,6 +160,8 @@
         return 0
 
     lax.fori_loop(0, groups, stats, 0)
+    for g in range(groups - 2, groups):
+        x_copy(g).start()
 
     def place(owner_static, block):
         wfull[owner_static * rows:(owner_static + 1) * rows, :feat] = block.astype(F32)
@@ -212,33 +253,59 @@
     bias_part = jnp.sum(jnp.transpose(gacc[...]), axis=0, keepdims=True)
     loss_part = jnp.sum(lacc[...], keepdims=True)
     count_part = jnp.sum(cbuf[...], keepdims=True)
-    row_of = lax.broadcasted_iota(jnp.int32, (8, featp), 0)
-    extra = jnp.where(row_of == 0, bias_part, jnp.where(row_of == 1, loss_part, count_part))
+    at_row = lax.broadcasted_iota(jnp.int32, (8, LANES), 0)
+    tiles = featp // LANES
+    extra = jnp.where(at_row == tiles, loss_part, count_part)
+    for n in range(tiles):
+        extra = jnp.where(at_row == n, bias_part[:, n * LANES:(n + 1) * LANES], extra)
+    starts, total_rows = layout(rows, feat)
     full = jnp.transpose(acc[...])
     for k in range(ndp):
-        gsend[k, :rows, :] = full[k * rows:(k + 1) * rows, :]
-        gsend[k, rows_pad:, :] = extra
+        slot = gsend.at[k % inner_dp, k // inner_dp]
+        if rows % 16:
+            slot[...] = jnp.zeros(slot.shape, F32)
+        mine = full[k * rows:(k + 1) * rows]
+        for n in range(feat // LANES):
+            slot[starts[n]:starts[n] + rows, :] = mine[:, n * LANES:(n + 1) * LANES]
+        if feat % LANES:
+            slot[starts[-2]:starts[-2] + rows // 2, :] = jnp.concatenate(
+                [mine[:rows // 2, feat - LANES // 2:feat], mine[rows // 2:, feat - LANES // 2:feat]], axis=1)
+        slot[starts[-1]:, :] = extra
+
+    other = 1 - near
+
+    def p_copy(o):
+        to = lax.rem(far + o, outer_dp)
+        return pltpu.make_async_remote_copy(
+            src_ref=gsend.at[other, to], dst_ref=pairv.at[o], send_sem=pss.at[o], recv_sem=prs.at[o],
+            device_id=(far * inner_dp + other, mp), device_id_type=MESH)
 
     def g_copy(o):
-        to = lax.rem(dp + o, ndp)
+        to = lax.rem(far + o, outer_dp)
         return pltpu.make_async_remote_copy(
-            src_ref=gsend.at[to], dst_ref=grecv.at[o - 1],
-            send_sem=gss.at[o - 1], recv_sem=grs.at[o - 1],
-            device_id=(to, mp), device_id_type=MESH)
-
-    for o in range(1, ndp):
-        g_copy(o).start()
-    grad = gsend[dp, :rows, :]
-    sums = gsend[dp, rows_pad:, :]
-    for o in range(1, ndp):
+            src_ref=gmid.at[o - 1], dst_ref=grecv.at[o - 1], send_sem=gss.at[o - 1], recv_sem=grs.at[o - 1],
+            device_id=(to * inner_dp + near, mp), device_id_type=MESH)
+
+    order = list(range(1, outer_dp)) + [0]
+    for o in order:
+        p_copy(o).start()
+    for o in order:
+        p_copy(o).wait_recv()
+        pair = gsend[near, lax.rem(far + o, outer_dp)] + pairv[o]
+        if o:
+            gmid[o - 1] = pair
+            g_copy(o).start()
+    for o in range(1, outer_dp):
         g_copy(o).wait_recv()
-        grad = grad + grecv[o - 1, :rows, :]
-        sums = sums + grecv[o - 1, rows_pad:, :]
-    bias_grad = sums[0:1, :]
+        pair = pair + grecv[o - 1]
+    out_ref[...] = pair
+    grad = pair[:starts[-1]]
+    sums = pair[starts[-1]:]
+    bias_grad = sums[:tiles]
     square = jnp.sum(grad * grad, keepdims=True)
     bias_square = jnp.sum(bias_grad * bias_grad, keepdims=True)
-    row_of = lax.broadcasted_iota(jnp.int32, (8, LANES), 0)
-    fsend[...] = jnp.where(row_of == 0, square + bias_square * (1.0 / ndp), sums[1:2, :LANES])
+    lane = lax.broadcasted_iota(jnp.int32, (1, LANES), 1)
+    fsend[...] = jnp.where(lane == 0, square + bias_square * (1.0 / ndp), sums[tiles:tiles + 1, :])
 
     def f_copy(o):
         d = lax.rem(me + o, ntot)
@@ -255,22 +322,15 @@
         return 0
 
     lax.fori_loop(1, ntot, f_start, 0)
-    count = sums[2:3, :LANES]
     lax.fori_loop(1, ntot, f_wait, 0)
-    final = fsend[...] + jnp.sum(frecv[...], axis=0)
-    norm = jnp.sqrt(final[0:1, :]) / count
-    scale = jnp.minimum(1.0, 1.0 / (norm + 1e-06))
-    factor = scale / count
-    loss = final[1:2, :] / count * (1.0 / (feat_full * ndp))
-    loss_ref[...] = loss
-    clip_ref[...] = scale
-    wide = jnp.concatenate([factor] * (featp // LANES), axis=1)
-    gw_ref[...] = (grad * wide)[:, :feat]
-    gb_ref[...] = (bias_grad * wide)[:, :feat]
+    fin_ref[...] = fsend[...] + jnp.sum(frecv[...], axis=0)
 
     for o in range(1, ndp):
         w_copy(o).wait_send()
-        g_copy(o).wait_send()
+    for o in order:
+        p_copy(o).wait_send()
+        if o:
+            g_copy(o).wait_send()
 
     def s_drain(g, _):
         for o in range(1, nmp):
@@ -293,21 +353,21 @@
     ndp, nmp = lax.axis_size("dp"), lax.axis_size("mp")
     ntot = ndp * nmp
     featp = pad_to(feat, LANES)
-    rows_pad = pad_to(rows, 8)
     groups = images // GROUP
     dma = pltpu.SemaphoreType.DMA
     vmem = pl.BlockSpec(memory_space=pltpu.VMEM)
     hbm = pl.BlockSpec(memory_space=pl.ANY)
-    loss, clip, gw, gb = pl.pallas_call(
+    _, total_rows = layout(rows, feat)
+    inner_dp = 2
+    outer_dp = ndp // inner_dp
+    summed, final = pl.pallas_call(
         functools.partial(kernel, ndp, nmp),
         out_shape=(
+            jax.ShapeDtypeStruct((total_rows, LANES), F32),
             jax.ShapeDtypeStruct((1, LANES), F32),
-            jax.ShapeDtypeStruct((1, LANES), F32),
-            jax.ShapeDtypeStruct((rows, feat), F32),
-            jax.ShapeDtypeStruct((1, feat), F32),
         ),
         in_specs=[hbm, vmem, vmem, hbm, hbm],
-        out_specs=(vmem,) * 4,
+        out_specs=(vmem,) * 2,
         scratch_shapes=[
             pltpu.VMEM((images * patches, width), BF16),
             pltpu.VMEM((images, feat, patches), BF16),
@@ -329,14 +389,17 @@
             pltpu.VMEM((featp, width), F32),
             pltpu.VMEM((featp, LANES), F32),
             pltpu.VMEM((CHUNK, patches), F32),
-            pltpu.VMEM((ndp, rows_pad + 8, featp), F32),
-            pltpu.VMEM((ndp - 1, rows_pad + 8, featp), F32),
-            pltpu.VMEM((8, LANES), F32),
-            pltpu.VMEM((ntot - 1, 8, LANES), F32),
+            pltpu.VMEM((inner_dp, outer_dp, total_rows, LANES), F32),
+            pltpu.VMEM((outer_dp, total_rows, LANES), F32),
+            pltpu.VMEM((outer_dp - 1, total_rows, LANES), F32),
+            pltpu.VMEM((outer_dp - 1, total_rows, LANES), F32),
+            pltpu.VMEM((1, LANES), F32),
+            pltpu.VMEM((ntot - 1, 1, LANES), F32),
             dma((groups,)), dma((groups,)), dma(()),
             dma((ndp - 1,)), dma((ndp - 1,)),
             dma((nmp - 1, groups)), dma((nmp - 1, groups)),
-            dma((ndp - 1,)), dma((ndp - 1,)),
+            dma((outer_dp,)), dma((outer_dp,)),
+            dma((outer_dp - 1,)), dma((outer_dp - 1,)),
             dma((ntot - 1,)), dma((ntot - 1,)),
         ],
         compiler_params=pltpu.CompilerParams(
@@ -349,7 +412,18 @@
         jnp.swapaxes(targets, 1, 2),
         block_masks,
     )
-    return loss[0, 0], clip[0, 0], gw, gb.reshape(feat)
+    loss, clip, gw, gb = pl.pallas_call(
+        functools.partial(finish, ndp, nmp),
+        out_shape=(
+            jax.ShapeDtypeStruct((1, 1), F32),
+            jax.ShapeDtypeStruct((1, 1), F32),
+            jax.ShapeDtypeStruct((rows, feat), F32),
+            jax.ShapeDtypeStruct((1, feat), F32),
+        ),
+        in_specs=[vmem] * 2,
+        out_specs=(vmem,) * 4,
+    )(summed, final)
+    return loss.reshape(()), clip.reshape(()), gw, gb.reshape(feat)
 
 
 def solution(mesh):

time: 67.3 us -> 56.2 us (0.84)
  Pallas kernels: 58.8 us -> 52.8 us
  between operations: 4.15 us -> 0.64 us
  local copies, waits for them, and re-layouts: 2.77 us -> 1.25 us
    pallas_call x1, Pallas kernels: 58.8 us -> 51.2 us  [body(): pl.pallas_call(functools.partial(kernel, ndp, nmp), out_shape=(jax.ShapeD...]
    pallas_call x0 -> x1, Pallas kernels: none -> 1.64 us  [body(): pl.pallas_call(functools.partial(finish, ndp, nmp), out_shape=(jax.ShapeD...]
    unnamed x1 -> x0, local copies, waits for them, and re-layouts: 1.52 us -> none
where the time goes in v2:
time: 56.2 us; the launch traced here: 55.9 us
  Pallas kernels  52.8 us (94%)
  local copies, waits for them, and re-layouts  1.25 us (2%)
  other arithmetic  1.23 us (2%)
  between operations  0.64 us (1%)
    pallas_call x1, Pallas kernels, body(): pl.pallas_call(functools.partial(kernel, ndp, nmp), out_shape=(jax.ShapeD...  51.2 us
    pallas_call x1, Pallas kernels, body(): pl.pallas_call(functools.partial(finish, ndp, nmp), out_shape=(jax.ShapeD...  1.64 us
    reshape x1, local copies, waits for them, and re-layouts, body(): proj_bias.reshape(1, feat)  1.25 us
    pallas_call x1, other arithmetic, body(): pl.pallas_call(functools.partial(finish, ndp, nmp), out_shape=(jax.ShapeD...  1.23 us

profile of v2, /device:TPU:0, one launch (start us, length us, event | category | flops | bytes accessed | tf_op | source)
XLA Modules:
  0.0 55.9 jit_solution(4481034228040602231)
XLA Ops:
  0.6 1.2 %reshape.24.b_ref = f32[1,320]{1,0:T(1,128)} reshape(f32[320]{0:T(512)} %param.7) | data formatting | bytes 2560 | tf_op jit(solution)/shard_map/reshape | solution.py:411
  1.9 51.2 %shard_map.84 = (f32[128,128]{1,0:T(8,128)}, f32[1,128]{1,0:T(1,128)}) custom-call(bf16[16384,384]{1,0:T(8,128)(2,1)} %bitcast.4, bf16[48,320]{1,0:T(8,128)(2,1)} %w_ref.1, f32[1,320]{1,0:T(1,128)} %reshape.24.b_ref, bf16[64,320,256]{2,1,0:T(8,128)(2,1)} %bitcast.5, s32[64,4,256]{2,1,0:T(4,128)} %m_hbm.1), custom_call_target="tpu_custom_call" | custom-call | tf_op jit(solution)/shard_map/pallas_call | solution.py:363
  53.1 1.6 %shard_map.85 = (f32[1,1]{1,0:T(1,128)}, f32[1,1]{1,0:T(1,128)}, f32[48,320]{1,0:T(8,128)}, f32[1,320]{1,0:T(1,128)}) custom-call(f32[128,128]{1,0:T(8,128)} %get-tuple-element.10.sum_ref, f32[1,128]{1,0:T(1,128)} %get-tuple-element.11.fin_ref), custom_call_target="tpu_custom_call" | custom-call | tf_op jit(solution)/shard_map/pallas_call | solution.py:415
  54.7 1.2 %reduce = f32[320]{0:T(512)} reduce(f32[1,320]{1,0:T(1,128)} %get-tuple-element.15, f32[]{:T(128)} %constant), dimensions={0}, to_apply=%get-tuple-element.15.reduce_sub_computation | reduce | bytes 2564 | tf_op jit(solution)/shard_map/pallas_call | solution.py:415

commit v3 on v2

--- a/solution.py
+++ b/solution.py
@@ -53,7 +53,7 @@
     for n in range(tiles):
         stop = min((n + 1) * LANES, feat)
         bias = sum_ref[starts[-1] + n:starts[-1] + n + 1, :] * factor
-        gb_ref[:, n * LANES:stop] = bias[:, :stop - n * LANES]
+        gb_ref[n * LANES:stop] = bias[0, :stop - n * LANES]
 
 
 def kernel(ndp, nmp, x_hbm, w_ref, b_ref, t_hbm, m_hbm,
@@ -86,22 +86,23 @@
 
     barrier = pltpu.get_barrier_semaphore()
 
+    for g in range(groups):
+        t_copy(g).start()
+    m_copy.start()
+
     def greet(o, _):
         d = lax.rem(me + o, ntot)
         pl.semaphore_signal(barrier, inc=1, device_id=(d // nmp, lax.rem(d, nmp)), device_id_type=MESH)
         return 0
 
     lax.fori_loop(1, ntot, greet, 0)
-    m_copy.start()
-    for g in range(groups):
-        t_copy(g).start()
     acc[...] = jnp.zeros_like(acc)
     gacc[...] = jnp.zeros_like(gacc)
     lacc[...] = jnp.zeros_like(lacc)
     sb[...] = jnp.zeros_like(sb)
     wfull[...] = jnp.zeros_like(wfull)
     brow[...] = jnp.zeros_like(brow)
-    brow[0:1, :feat] = b_ref[...]
+    brow[0:1, :feat] = b_ref[...].reshape(1, feat)
     bcol[...] = jnp.transpose(jnp.broadcast_to(brow[0:1, :], (LANES, featp)))
 
     pl.semaphore_wait(barrier, ntot - 1)
@@ -408,7 +409,7 @@
     )(
         pred_input.reshape(images * patches, width),
         proj_weight,
-        proj_bias.reshape(1, feat),
+        proj_bias,
         jnp.swapaxes(targets, 1, 2),
         block_masks,
     )
@@ -418,12 +419,12 @@
             jax.ShapeDtypeStruct((1, 1), F32),
             jax.ShapeDtypeStruct((1, 1), F32),
             jax.ShapeDtypeStruct((rows, feat), F32),
-            jax.ShapeDtypeStruct((1, feat), F32),
+            jax.ShapeDtypeStruct((feat,), F32),
         ),
         in_specs=[vmem] * 2,
         out_specs=(vmem,) * 4,
     )(summed, final)
-    return loss.reshape(()), clip.reshape(()), gw, gb.reshape(feat)
+    return loss.reshape(()), clip.reshape(()), gw, gb
 
 
 def solution(mesh):

time: 56.2 us -> 53.9 us (0.959)
  local copies, waits for them, and re-layouts: 1.25 us -> 0 us
  other arithmetic: 1.23 us -> 0 us
    reshape x1 -> x0, local copies, waits for them, and re-layouts: 1.25 us -> none  [body(): proj_bias.reshape(1, feat)]
    pallas_call x1 -> x0, other arithmetic: 1.23 us -> none  [body(): pl.pallas_call(functools.partial(finish, ndp, nmp), out_shape=(jax.ShapeD...]
where the time goes in v3:
time: 53.9 us; the launch traced here: 53.7 us
  Pallas kernels  53 us (98%)
  between operations  0.64 us (1%)
    pallas_call x1, Pallas kernels, body(): pl.pallas_call(functools.partial(kernel, ndp, nmp), out_shape=(jax.ShapeD...  51.4 us
    pallas_call x1, Pallas kernels, body(): pl.pallas_call(functools.partial(finish, ndp, nmp), out_shape=(jax.ShapeD...  1.64 us

profile of v3, /device:TPU:0, one launch (start us, length us, event | category | flops | bytes accessed | tf_op | source)
XLA Modules:
  0.0 53.7 jit_solution(10588443647334156837)
XLA Ops:
  0.6 51.4 %shard_map.84 = (f32[128,128]{1,0:T(8,128)}, f32[1,128]{1,0:T(1,128)}) custom-call(bf16[16384,384]{1,0:T(8,128)(2,1)} %bitcast.4, bf16[48,320]{1,0:T(8,128)(2,1)} %w_ref.1, f32[320]{0:T(512)} %b_ref.1, bf16[64,320,256]{2,1,0:T(8,128)(2,1)} %bitcast.5, s32[64,4,256]{2,1,0:T(4,128)} %m_hbm.1), custom_call_target="tpu_custom_call" | custom-call | tf_op jit(solution)/shard_map/pallas_call | solution.py:364
  52.0 1.6 %shard_map.85 = (f32[1,1]{1,0:T(1,128)}, f32[1,1]{1,0:T(1,128)}, f32[48,320]{1,0:T(8,128)}, f32[320]{0:T(512)}) custom-call(f32[128,128]{1,0:T(8,128)} %get-tuple-element.10.sum_ref, f32[1,128]{1,0:T(1,128)} %get-tuple-element.11.fin_ref), custom_call_target="tpu_custom_call" | custom-call | tf_op jit(solution)/shard_map/pallas_call | solution.py:416
